TPU v7x, 32 devices: a whole 2x2x4 slice. The times are simulated.
32 devices in a mesh: rows: 8 (over z, x), grp: 4 (over y, core).
Axes of the slice: x: 2, y: 2, z: 4, core: 2. Of those that a mesh axis runs over, the one named last changes fastest.
Arguments:
- matrix: bfloat16 [10240, 16384], P(('rows', 'grp')), may hold values from -36 to 36
- sample_rows: int32 [32, 128, 256], P(('rows', 'grp')), may hold values from 0 to 319
- pair_list: int32 [8, 8, 4], replicated, may hold values from 0 to 255, as said below
- pair_count: int32 [8, 8], replicated, may hold values from 1 to 4, as said below
- pair_blocks: int32 [256, 2], replicated, may hold values from 0 to 127, as said below
Outputs:
- gram: float32 [256, 128, 128], P(('rows', 'grp'))
Inputs may be any that keep to these rules, and one draw needn't show every extreme that they name: `pair_list`: entry [s, r, k] lies in [r * 32, (r + 1) * 32); the 4 entries of one [s, r] are distinct. `pair_count`: every row group has some owner with all 4 slots active, and some owner has all 4 slots active from every row group. `pair_blocks`: the two blocks of a pair differ.
All inputs are finite; a program needn't handle non-finite values.
Results may differ from a plain program's by a relative error of at most 0.0016.
Values sent between devices are 32-bit elements; how exact they have to be, the bound alone decides.
A program may use at most 192 MiB of HBM per device.

v0:
```python
import math

import jax
import jax.numpy as jnp
from jax import lax
from jax.sharding import PartitionSpec as P

epsilon = 1e-06


def shards(matrix, sample_rows, pair_list, pair_count, pair_blocks):
    rows_dev, column_count = matrix.shape
    block_count = sample_rows.shape[1]
    sample_count = sample_rows.shape[2]
    width = column_count // block_count
    row_axis_size = lax.axis_size("rows")
    grp_axis_size = lax.axis_size("grp")
    slot_cap = pair_list.shape[2]
    region_size = pair_blocks.shape[0] // row_axis_size
    row_index = lax.axis_index("rows")
    grp_index = lax.axis_index("grp")
    squares = jnp.sum(jnp.square(matrix.astype(jnp.float32)), axis=0)
    column_total = lax.psum(squares, ("rows", "grp"))
    root_mean = jnp.sqrt(column_total / (rows_dev * row_axis_size * grp_axis_size) + epsilon)
    positions = lax.iota(jnp.int32, rows_dev)
    picked = sample_rows[0]
    multiplicity = jnp.sum(
        (picked[:, :, None] == positions[None, None, :]).astype(jnp.float32), axis=1
    )
    blocks = matrix.reshape(rows_dev, block_count, width)
    weighted = (jnp.transpose(multiplicity)[:, :, None] * blocks.astype(jnp.float32)).astype(
        jnp.bfloat16
    )
    my_pairs = pair_list[row_index]
    my_counts = pair_count[row_index]
    live_mask = (lax.iota(jnp.int32, slot_cap)[None, :] < my_counts[:, None]).astype(jnp.float32)
    pair_ids = my_pairs.reshape(-1)
    slot_total = pair_ids.shape[0]
    group_size = math.gcd(32, slot_total)
    first_block = jnp.take(pair_blocks[:, 0], pair_ids).reshape(-1, group_size)
    second_block = jnp.take(pair_blocks[:, 1], pair_ids).reshape(-1, group_size)

    def tile_group(block_pair):
        weighted_cols = jnp.take(weighted, block_pair[0], axis=1)
        plain_cols = jnp.take(blocks, block_pair[1], axis=1)
        return jnp.einsum(
            "rgi,rgj->gij", weighted_cols, plain_cols, preferred_element_type=jnp.float32
        )

    partial_tiles = lax.map(tile_group, (first_block, second_block))
    partial_tiles = (
        partial_tiles.reshape(row_axis_size, slot_cap, width, width) * live_mask[:, :, None, None]
    )
    received = lax.all_to_all(partial_tiles, "rows", split_axis=0, concat_axis=0, tiled=True)
    source_ids = pair_list[:, row_index, :]
    local_ids = source_ids.reshape(-1) - row_index * region_size
    select_matrix = (lax.iota(jnp.int32, region_size)[:, None] == local_ids[None, :]).astype(
        jnp.float32
    )
    flat_received = received.reshape(local_ids.shape[0], width * width)
    owner_tiles = jnp.dot(
        select_matrix,
        flat_received,
        precision=lax.Precision.HIGHEST,
        preferred_element_type=jnp.float32,
    )
    owned_tiles = lax.psum_scatter(
        owner_tiles.reshape(region_size, width, width), "grp", scatter_dimension=0, tiled=True
    )
    tile_dev = owned_tiles.shape[0]
    owned_pairs = (row_index * grp_axis_size + grp_index) * tile_dev + lax.iota(jnp.int32, tile_dev)
    owned_blocks = jnp.take(pair_blocks, owned_pairs, axis=0)
    scale_blocks = root_mean.reshape(block_count, width)
    left_scale = jnp.take(scale_blocks, owned_blocks[:, 0], axis=0)
    right_scale = jnp.take(scale_blocks, owned_blocks[:, 1], axis=0)
    return owned_tiles / (sample_count * left_scale[:, :, None] * right_scale[:, None, :])


def solution(mesh):
    in_specs = (P(("rows", "grp"), None), P(("rows", "grp"), None, None), P(), P(), P())
    out_specs = P(("rows", "grp"), None, None)
    return jax.shard_map(shards, mesh=mesh, in_specs=in_specs, out_specs=out_specs, check_vma=False)
```

profile of v0, /device:TPU:0, one launch (start us, length us, event | category | flops | bytes accessed | tf_op | source)
XLA Modules:
  0.0 224.8 jit_solution(7144208598119614567)
XLA Ops:
  7.4 0.7 constant_dynamic-slice_fusion.1
  8.2 0.8 fusion.18
  9.0 0.7 gather_fusion.1
  9.7 0.7 gather_fusion.3
  10.4 9.4 %convert_reduce_fusion = f32[128,320]{1,0:T(8,128)S(1)} fusion(s32[128,256]{1,0:T(8,128)} %bitcast.48), kind=kLoop, calls=%fused_computation.7 | loop fusion | flops 31416320 | bytes 294912 | tf_op jit(solution)/shard_map/reduce_sum | solution.py:27
  19.8 11.0 %copy_bitcast_fusion = bf16[320,128,128]{2,0,1:T(8,128)(2,1)} fusion(bf16[320,16384]{1,0:T(8,128)(2,1)} %param.11), kind=kLoop, calls=%fused_computation.11 | loop fusion | bytes 20971520 | tf_op jit(solution)/shard_map/reshape | solution.py:30
  30.8 10.0 %multiply_convert_fusion = bf16[320,128,128]{2,0,1:T(8,128)(2,1)} fusion(f32[320,128]{0,1:T(8,128)S(1)} %bitcast.47, bf16[320,16384]{1,0:T(8,128)(2,1)} %param.11), kind=kLoop, calls=%fused_computation.10 | loop fusion | flops 15728640 | bytes 21135360 | tf_op jit(solution)/shard_map/convert_element_type | solution.py:31
  40.9 5.0 %gather_fusion.2 = bf16[32,320,128]{2,1,0:T(8,128)(2,1)S(1)} fusion(bf16[320,128,128]{2,0,1:T(8,128)(2,1)} %multiply_convert_fusion, s32[1024]{0:T(1024)S(1)} %get-tuple-element.39), kind=kCustom, calls=%fused_computation.1.clone | custom fusion | bytes 5243008 | tf_op jit(solution)/shard_map/while/body/eval_jaxpr/jit(_take)/gather | solution.py:44
  45.9 6.4 %gather_fusion.4 = bf16[32,320,128]{2,1,0:T(8,128)(2,1)} fusion(bf16[320,128,128]{2,0,1:T(8,128)(2,1)} %copy_bitcast_fusion, s32[1024]{0:T(1024)S(1)} %get-tuple-element.38), kind=kCustom, calls=%fused_computation.4.clone | custom fusion | bytes 5243008 | tf_op jit(solution)/shard_map/while/body/eval_jaxpr/jit(_take)/gather | solution.py:45
  52.3 3.0 %fusion = f32[32,128,128]{2,1,0:T(8,128)S(1)} fusion(bf16[32,320,128]{2,1,0:T(8,128)(2,1)} %gather_fusion.4, bf16[32,320,128]{2,1,0:T(8,128)(2,1)S(1)} %gather_fusion.2, pred[32]{0:T(512)(128)(4,1)S(1)} %get-tuple-element.34, pred[32]{0:T(512)(128)(4,1)S(1)} %get-tuple-element.28), kind=kOutput, calls=%fused_computation.12 | convolution fusion | flops 338165760 | bytes 7340096 | tf_op jit(solution)/shard_map/while/body/eval_jaxpr/rgi,rgj->gij/dot_general | solution.py:46
  55.3 1.6 broadcast_multiply_fusion
  56.9 7.3 %all-to-all-start = ((f32[8,4,128,128]{3,2,1,0:T(8,128)}), f32[8,4,128,128]{3,2,1,0:T(8,128)S(1)}, u32[]{:S(2)}, u32[]{:S(2)}) async-start(f32[8,4,128,128]{3,2,1,0:T(8,128)} %broadcast_multiply_fusion), calls=%async_computation | async-start | bytes 4194304 | tf_op jit(solution)/shard_map/all_to_all | solution.py:54
  64.2 6.8 %multiply_reduce_fusion = f32[16384]{0:T(1024)} fusion(bf16[320,16384]{1,0:T(8,128)(2,1)} %param.11), kind=kLoop, calls=%fused_computation.9 | loop fusion | flops 15712256 | bytes 10551296 | tf_op jit(solution)/shard_map/reduce_sum | solution.py:22
  71.0 0.2 reduce-scatter.2.cloned.1.call-start
  71.2 0.3 subtract_reduce_fusion
  71.6 41.3 %all-to-all-done = f32[8,4,128,128]{3,2,1,0:T(8,128)S(1)} async-done(((f32[8,4,128,128]{3,2,1,0:T(8,128)}), f32[8,4,128,128]{3,2,1,0:T(8,128)S(1)}, u32[]{:S(2)}, u32[]{:S(2)}) %all-to-all-start) | async-done | bytes 2097184 | tf_op jit(solution)/shard_map/all_to_all | solution.py:54
  112.9 3.8 %fusion.7 = f32[32,128,128]{2,0,1:T(8,128)} fusion(s32[32]{0:T(128)S(1)} %sub.15, f32[4,8,128,128]{3,2,1,0:T(8,128)S(1)} %bitcast.45), kind=kOutput, calls=%fused_computation.20 | convolution fusion | flops 201327616 | bytes 4194432 | tf_op jit(solution)/shard_map/dot_general | solution.py:61
  116.9 0.6 gather_fusion
  117.8 95.2 %all-reduce.2.cloned.1.call-done = f32[16384]{0:T(1024)} async-done(((f32[16384]{0:T(1024)}), f32[16384]{0:T(1024)}) %all-reduce.2.cloned.1.call-update) | async-done | bytes 65552 | tf_op jit(solution)/shard_map/psum | solution.py:23
  213.0 0.9 sqrt_bitcast_fusion
  213.9 0.6 gather_fusion.5
  214.6 0.6 gather_fusion.6
  215.2 1.2 multiply_divide_fusion
  216.5 0.9 copy.28
  (33 shorter events, 1.1 us)
Async XLA Ops:
  7.4 33.4 %copy-start = (s32[8,8]{1,0:T(8,128)S(1)}, s32[8,8]{1,0:T(8,128)}, u32[]{:S(2)}) copy-start(s32[8,8]{1,0:T(8,128)} %param.14) | copy-start | bytes 772
  56.9 56.1 %all-to-all-start = ((f32[8,4,128,128]{3,2,1,0:T(8,128)}), f32[8,4,128,128]{3,2,1,0:T(8,128)S(1)}, u32[]{:S(2)}, u32[]{:S(2)}) async-start(f32[8,4,128,128]{3,2,1,0:T(8,128)} %broadcast_multiply_fusion), calls=%async_computation | async-start | bytes 4194304 | tf_op jit(solution)/shard_map/all_to_all | solution.py:54
  64.1 7.1 %copy-start.1 = (s32[8,8,4]{1,2,0:T(4,128)S(1)}, s32[8,8,4]{1,2,0:T(4,128)}, u32[]{:S(2)}) copy-start(s32[8,8,4]{1,2,0:T(4,128)} %param.13) | copy-start | bytes 3076
  64.2 148.9 %all-reduce.2.cloned.1.call-start = ((), (), s32[]{:S(2)}) async-start(), calls=%async_computation.3 | async-start | bytes 131072 | tf_op jit(solution)/shard_map/psum | solution.py:23
  71.0 144.3 %reduce-scatter.2.cloned.1.call-start = ((), (), s32[]{:S(2)}) async-start(), calls=%async_computation.2 | async-start | bytes 2621440 | tf_op jit(solution)/shard_map/reduce_scatter | solution.py:67
  112.9 3.8 %copy-start.2 = (s32[256,2]{0,1:T(2,128)S(1)}, s32[256,2]{0,1:T(2,128)}, u32[]{:S(2)}) copy-start(s32[256,2]{0,1:T(2,128)} %param.15) | copy-start | bytes 6148
Sparse Core Ops, SparseCore 0:
  71.1 141.8 all-reduce.1
Sparse Core Ops, SparseCore 1:
  116.8 30.3 reduce-scatter.1
where the time goes:
time: 227 us; the launch traced here: 225 us
  waiting for transfers between devices  137 us (60%)
  other arithmetic  30.4 us (13%)
  local copies, waits for them, and re-layouts  28.5 us (13%)
  between operations  15 us (7%)
  starting transfers between devices  7.55 us (3%)
  matrix products  6.78 us (3%)
    psum x1, waiting for transfers between devices, shards(): column_total = lax.psum(squares, ('rows', 'grp'))  95.2 us
    all_to_all x1, waiting for transfers between devices, shards(): lax.all_to_all(partial_tiles, 'rows', split_axis=0, concat_axis=0, tiled=...  41.3 us
    reshape x1, local copies, waits for them, and re-layouts, shards(): blocks = matrix.reshape(rows_dev, block_count, width)  11 us
    convert_element_type x1, other arithmetic, shards(): (jnp.transpose(multiplicity)[:, :, None] * blocks.astype(jnp.float32)).as...  10 us
    reduce_sum x1, other arithmetic, shards(): jnp.sum((picked[:, :, None] == positions[None, None, :]).astype(jnp.float...  9.36 us
    all_to_all x1, starting transfers between devices, shards(): lax.all_to_all(partial_tiles, 'rows', split_axis=0, concat_axis=0, tiled=...  7.28 us
    reduce_sum x1, other arithmetic, shards(): squares = jnp.sum(jnp.square(matrix.astype(jnp.float32)), axis=0)  6.75 us
    gather x1, local copies, waits for them, and re-layouts, tile_group(): plain_cols = jnp.take(blocks, block_pair[1], axis=1)  6.38 us
  transfers between devices with their start and end apart: 3, of which 2 were waited for; matrix products, arithmetic and copies ran while one was open for 6% of the time, Pallas kernels for 0%

commit v1 on v0

v1 whole, which is shorter than its diff:
```python
import functools

import jax
import jax.numpy as jnp
from jax import lax
from jax.experimental import pallas as pl
from jax.experimental.pallas import tpu as pltpu
from jax.sharding import PartitionSpec as P

epsilon = 1e-06
MESH = pl.DeviceIdType.MESH
F32 = jnp.float32
BF16 = jnp.bfloat16


def kernel(
    dims, table, samples, matrix, out,
    mat, squares, sq_in, sq_half, sq_in2, sq_rows, sq_total,
    core_out, core_in, keep, row_in, part_a, part_b, part_c, part_d, in_a, in_b, in_c,
    load_sem, sq_send, sq_recv, sq_row_send, sq_row_recv,
    core_send, core_recv, row_send, row_recv,
    a_send, a_recv, b_send, b_recv, c_send, c_recv,
):
    row_count, grp_count, cap, pairs = dims
    block_count, rows_dev, width = mat.shape
    sample_count = samples.shape[1]
    half = cap // 2
    region = pairs // row_count
    tile_dev = region // grp_count
    count_at = row_count * row_count * cap
    first_at = count_at + row_count * row_count
    second_at = first_at + pairs

    s = lax.axis_index("rows")
    g = lax.axis_index("grp")
    low = lax.rem(g, 2)
    high = lax.div(g, 2)
    partner = high * 2 + (1 - low)
    across = (1 - high) * 2 + low

    def at(row, grp):
        return {"rows": row, "grp": grp}

    def send(source, target, send_sem, recv_sem, row, grp):
        return pltpu.make_async_remote_copy(
            src_ref=source, dst_ref=target, send_sem=send_sem, recv_sem=recv_sem,
            device_id=at(row, grp), device_id_type=MESH,
        )

    def load(i):
        source = matrix.at[:, pl.ds(pl.multiple_of(i * width, width), width)]
        return pltpu.make_async_copy(source, mat.at[i], load_sem.at[i])

    def load_go(i, carry):
        load(i).start()
        return carry

    lax.fori_loop(0, block_count, load_go, 0)

    barrier = pltpu.get_barrier_semaphore()
    pl.semaphore_signal(barrier, inc=1, device_id=at(s, partner), device_id_type=MESH)
    pl.semaphore_signal(barrier, inc=1, device_id=at(s, across), device_id_type=MESH)

    def greet(j, carry):
        row = lax.rem(s + j, row_count)
        pl.semaphore_signal(barrier, inc=1, device_id=at(row, g), device_id_type=MESH)
        return carry

    lax.fori_loop(1, row_count, greet, 0)

    zero_tile = jnp.zeros((width, width), F32)

    def clear(j, carry):
        row_in[j, half] = zero_tile
        return carry

    lax.fori_loop(0, row_count, clear, 0)

    def square_group(n, carry):
        lines = []
        for m in range(8):
            load(n * 8 + m).wait()
        for m in range(8):
            values = mat[n * 8 + m].astype(F32)
            lines.append(jnp.sum(values * values, axis=0, keepdims=True))
        squares[pl.ds(pl.multiple_of(n * 8, 8), 8), :] = jnp.concatenate(lines, axis=0)
        return carry

    lax.fori_loop(0, block_count // 8, square_group, 0)
    pl.semaphore_wait(barrier, row_count + 1)

    nb2 = block_count // 2
    nb4 = block_count // 4

    def span(start, size):
        return pl.ds(pl.multiple_of(start, 8), size)

    sq1 = send(squares.at[span((1 - low) * nb2, nb2)], sq_in, sq_send.at[0], sq_recv.at[0], s, partner)
    sq2 = send(sq_half.at[span((1 - high) * nb4, nb4)], sq_in2, sq_send.at[1], sq_recv.at[1], s, across)
    quarter = span(low * nb2 + high * nb4, nb4)
    sq4 = send(sq_total.at[quarter], sq_total.at[quarter], sq_send.at[2], sq_recv.at[2], s, across)
    my_half = span(low * nb2, nb2)
    sq5 = send(sq_total.at[my_half], sq_total.at[my_half], sq_send.at[3], sq_recv.at[3], s, partner)

    def sq_row(j):
        row = lax.rem(s + j, row_count)
        return send(sq_rows.at[s], sq_rows.at[s], sq_row_send.at[j], sq_row_recv.at[s], row, g)

    def sq_row_from(j):
        source = lax.rem(s + j, row_count)
        return send(sq_rows.at[source], sq_rows.at[source], sq_row_send.at[j], sq_row_recv.at[source], source, g)

    positions = lax.broadcasted_iota(jnp.int32, (rows_dev, sample_count), 0)
    ones = jnp.ones((sample_count, width), BF16)

    def slot_tile(owner, slot):
        pair = table[(s * row_count + owner) * cap + slot]
        active = (slot < table[count_at + s * row_count + owner]).astype(F32)
        first = table[first_at + pair]
        second = table[second_at + pair]
        picked = samples[first].reshape(1, sample_count)
        hits = jnp.where(positions == picked, 1.0, 0.0).astype(BF16)
        multiplicity = jnp.dot(hits, ones, preferred_element_type=F32)
        left = mat[first].astype(F32)
        right = mat[second]
        weighted = (multiplicity * active * left).astype(BF16)
        return lax.dot_general(
            weighted, right, (((0,), (0,)), ((), ())), preferred_element_type=F32
        )

    def core_copy(j):
        return send(core_out.at[j], core_in.at[j], core_send.at[j], core_recv.at[j], s, partner)

    def row_copy(j):
        owner = lax.rem(s + j, row_count)
        target = row_in.at[s, pl.ds(0, half)]
        return send(keep.at[j], target, row_send.at[j], row_recv.at[s], owner, g)

    def row_from(j):
        source = lax.rem(s + j, row_count)
        target = row_in.at[source, pl.ds(0, half)]
        return send(keep.at[j], target, row_send.at[j], row_recv.at[source], source, g)

    def make(j):
        owner = lax.rem(s + j, row_count)
        for n in range(half):
            core_out[j, n] = slot_tile(owner, (1 - low) * half + n)
        core_copy(j).start()
        for n in range(half):
            keep[j, n] = slot_tile(owner, low * half + n)

    def forward(j):
        core_copy(j).wait_recv()
        keep[j] = keep[j] + core_in[j]
        row_copy(j).start()

    def step(j, carry):
        make(j)
        forward(j - 1)
        return carry

    cut1 = min(3, row_count)
    cut2 = min(5, row_count)
    sq1.start()
    make(1)
    lax.fori_loop(2, cut1, step, 0)
    sq1.wait()
    sq_half[...] = squares[my_half, :] + sq_in[...]
    sq2.start()
    lax.fori_loop(cut1, cut2, step, 0)
    sq2.wait()
    sq_rows[s] = sq_half[span(high * nb4, nb4), :] + sq_in2[...]

    def sq_go(j, carry):
        sq_row(j).start()
        return carry

    lax.fori_loop(1, row_count, sq_go, 0)
    lax.fori_loop(cut2, row_count, step, 0)
    make(0)
    forward(row_count - 1)
    core_copy(0).wait_recv()
    row_in[s, pl.ds(0, half)] = keep[0] + core_in[0]

    def sq_done(j, carry):
        sq_row_from(j).wait_recv()
        return carry

    lax.fori_loop(1, row_count, sq_done, 0)
    sq_sum = sq_rows[0]
    for j in range(1, row_count):
        sq_sum = sq_sum + sq_rows[j]
    sq_total[quarter, :] = sq_sum
    sq4.start()

    def row_done(j, carry):
        row_from(j).wait_recv()
        return carry

    lax.fori_loop(1, row_count, row_done, 0)

    def owned(grp, n):
        pair = s * region + grp * tile_dev + n
        total = None
        for source in range(row_count):
            base = (source * row_count + s) * cap + low * half
            index = half
            for m in range(half):
                same = (table[base + m] == pair).astype(jnp.int32)
                index = jnp.minimum(index, half - (half - m) * same)
            tile = row_in[source, index]
            total = tile if total is None else total + tile
        return total

    def a_copy(n):
        return send(part_a.at[n], in_a.at[n], a_send.at[n], a_recv.at[n], s, partner)

    def b_copy(n):
        return send(part_b.at[n], in_b.at[n], b_send.at[n], b_recv.at[n], s, across)

    c_copy = send(part_c, in_c, c_send, c_recv, s, partner)
    far_low = (1 - high) * 2 + low
    far_other = (1 - high) * 2 + (1 - low)

    def pass_on(n):
        a_copy(n).wait_recv()
        part_b[n] = part_b[n] + in_a[n]
        b_copy(n).start()

    def far(n, carry):
        part_a[n] = owned(far_other, n)
        a_copy(n).start()
        part_b[n] = owned(far_low, n)

        @pl.when(n > 0)
        def _():
            pass_on(n - 1)

        return carry

    lax.fori_loop(0, tile_dev, far, 0)
    pass_on(tile_dev - 1)
    sq4.wait()
    sq5.start()

    def near_other(n, carry):
        part_c[n] = owned(partner, n)
        return carry

    lax.fori_loop(0, tile_dev, near_other, 0)
    c_copy.start()

    def near(n, carry):
        part_d[n] = owned(g, n)
        return carry

    lax.fori_loop(0, tile_dev, near, 0)
    sq5.wait()
    c_copy.wait()
    sq_total[...] = jnp.sqrt(
        sq_total[...] / (rows_dev * row_count * grp_count) + epsilon
    )

    def finish(n, carry):
        pair = s * region + g * tile_dev + n
        first = table[first_at + pair]
        second = table[second_at + pair]
        left = jnp.broadcast_to(sq_total[first].reshape(1, width), (width, width)).T
        right = sq_total[second].reshape(1, width)
        b_copy(n).wait_recv()
        total = part_d[n] + in_c[n] + in_b[n]
        out[n] = total / (sample_count * left * right)
        return carry

    lax.fori_loop(0, tile_dev, finish, 0)

    def drain_tiles(n, carry):
        a_copy(n).wait_send()
        b_copy(n).wait_send()
        return carry

    lax.fori_loop(0, tile_dev, drain_tiles, 0)

    def drain_rows(j, carry):
        core_copy(j).wait_send()
        row_copy(j).wait_send()
        sq_row(j).wait_send()
        return carry

    lax.fori_loop(1, row_count, drain_rows, 0)
    core_copy(0).wait_send()


def shards(matrix, sample_rows, pair_list, pair_count, pair_blocks):
    rows_dev, column_count = matrix.shape
    block_count, sample_count = sample_rows.shape[1:]
    width = column_count // block_count
    row_count = lax.axis_size("rows")
    grp_count = lax.axis_size("grp")
    cap = pair_list.shape[2]
    pairs = pair_blocks.shape[0]
    tile_dev = pairs // (row_count * grp_count)
    half = cap // 2
    table = jnp.concatenate(
        [
            pair_list.reshape(-1),
            pair_count.reshape(-1),
            pair_blocks[:, 0],
            pair_blocks[:, 1],
        ]
    )
    dma = pltpu.SemaphoreType.DMA

    def vmem(*shape):
        return pltpu.VMEM(shape, F32)

    some = vmem(tile_dev, width, width)
    nb2, nb4 = block_count // 2, block_count // 4
    return pl.pallas_call(
        functools.partial(kernel, (row_count, grp_count, cap, pairs)),
        out_shape=jax.ShapeDtypeStruct((tile_dev, width, width), F32),
        in_specs=[
            pl.BlockSpec(memory_space=pltpu.SMEM),
            pl.BlockSpec(memory_space=pltpu.VMEM),
            pl.BlockSpec(memory_space=pl.ANY),
        ],
        out_specs=pl.BlockSpec(memory_space=pltpu.VMEM),
        scratch_shapes=[
            pltpu.VMEM((block_count, rows_dev, width), BF16),
            vmem(block_count, width),
            vmem(nb2, width),
            vmem(nb2, width),
            vmem(nb4, width),
            vmem(row_count, nb4, width),
            vmem(block_count, width),
            vmem(row_count, half, width, width),
            vmem(row_count, half, width, width),
            vmem(row_count, half, width, width),
            vmem(row_count, half + 1, width, width),
            some, some, some, some, some, some, some,
            dma((block_count,)), dma((4,)), dma((4,)), dma((row_count,)), dma((row_count,)),
            dma((row_count,)), dma((row_count,)), dma((row_count,)), dma((row_count,)),
            dma((tile_dev,)), dma((tile_dev,)), dma((tile_dev,)), dma((tile_dev,)),
            dma, dma,
        ],
        compiler_params=pltpu.CompilerParams(
            collective_id=0, has_side_effects=True, vmem_limit_bytes=67043328
        ),
        name="gram_tiles",
    )(table, sample_rows[0], matrix)


def solution(mesh):
    in_specs = (P(("rows", "grp"), None), P(("rows", "grp"), None, None), P(), P(), P())
    out_specs = P(("rows", "grp"), None, None)
    return jax.shard_map(shards, mesh=mesh, in_specs=in_specs, out_specs=out_specs, check_vma=False)
```

time: 227 us -> 61.2 us (0.27)
  the two profiles are of different devices: /device:TPU:0 before, /device:TPU:11 now
where the time goes in v1:
time: 61.2 us; the launch traced here: 60.9 us
  Pallas kernels  55.9 us (91%)
  local copies, waits for them, and re-layouts  4.33 us (7%)
  other arithmetic  0.67 us (1%)
    pallas_call x1, Pallas kernels, shards(): pl.pallas_call(functools.partial(kernel, (row_count, grp_count, cap, pair...  55.9 us
    unnamed x2, local copies, waits for them, and re-layouts  2.7 us

profile of v1, /device:TPU:11, one launch (start us, length us, event | category | flops | bytes accessed | tf_op | source)
XLA Modules:
  0.0 60.9 jit_solution(13263063201822299253)
XLA Ops:
  0.0 0.8 %reshape.7 = s32[64]{0:T(128)S(1)} reshape(s32[8,8]{1,0:T(8,128)} %param.8) | data formatting | bytes 512 | tf_op jit(solution)/shard_map/reshape | solution.py:307
  0.8 0.8 %fusion = (s32[256,1]{0,1:T(1,128)S(1)}, s32[256,1]{0,1:T(1,128)S(1)}) fusion(s32[256,2]{0,1:T(2,128)} %param.9), kind=kLoop, calls=%fused_computation.1 | loop fusion | bytes 4096 | tf_op jit(solution)/shard_map/slice | solution.py:308
  1.5 0.8 %copy.6 = s32[8,8,4]{2,1,0:T(8,128)S(1)} copy(s32[8,8,4]{1,2,0:T(4,128)} %param.7) | data formatting | bytes 2048 | tf_op args[2]
  2.4 0.1 reshape.6
  2.5 0.7 %pad_add_fusion.table = s32[832]{0:T(1024)} fusion(s32[256]{0:T(256)S(1)} %bitcast.5, s32[256]{0:T(256)S(1)} %bitcast.4, s32[64]{0:T(128)S(1)} %reshape.7, s32[256]{0:T(256)S(1)} %reshape.6), kind=kLoop, calls=%fused_computation | loop fusion | flops 2496 | bytes 6656 | tf_op jit(solution)/shard_map/concatenate | solution.py:304
  3.1 55.9 %gram_tiles.1 = f32[8,128,128]{2,1,0:T(8,128)} custom-call(s32[832]{0:T(1024)} %pad_add_fusion.table, s32[128,256]{1,0:T(8,128)} %bitcast.3, bf16[320,16384]{1,0:T(8,128)(2,1)} %matrix.1), custom_call_target="tpu_custom_call" | custom-call | tf_op jit(solution)/shard_map/gram_tiles/pallas_call | solution.py:319
  59.0 1.9 %copy.8 = f32[8,128,128]{2,1,0:T(8,128)} copy(f32[8,128,128]{2,1,0:T(8,128)} %gram_tiles.1) | data formatting | bytes 1048576

commit v2 on v1

--- a/solution.py
+++ b/solution.py
@@ -14,11 +14,11 @@
 
 
 def kernel(
-    dims, table, samples, matrix, out,
-    mat, squares, sq_in, sq_half, sq_in2, sq_rows, sq_total,
-    core_out, core_in, keep, row_in, part_a, part_b, part_c, part_d, in_a, in_b, in_c,
+    dims, pair_list, pair_count, pair_blocks, samples_hbm, matrix, out,
+    mat, samples, sample_sem, squares, sq_in, sq_half, sq_in2, sq_rows, sq_total,
+    core_out, core_in, keep, high_in, row_in, part_a, part_b, part_c, part_d, in_a, in_b, in_c,
     load_sem, sq_send, sq_recv, sq_row_send, sq_row_recv,
-    core_send, core_recv, row_send, row_recv,
+    core_send, core_recv, high_send, high_recv, row_send, row_recv,
     a_send, a_recv, b_send, b_recv, c_send, c_recv,
 ):
     row_count, grp_count, cap, pairs = dims
@@ -27,9 +27,8 @@
     half = cap // 2
     region = pairs // row_count
     tile_dev = region // grp_count
-    count_at = row_count * row_count * cap
-    first_at = count_at + row_count * row_count
-    second_at = first_at + pairs
+    quota = half // 2
+    row_half = row_count // 2
 
     s = lax.axis_index("rows")
     g = lax.axis_index("grp")
@@ -55,6 +54,8 @@
         load(i).start()
         return carry
 
+    sample_load = pltpu.make_async_copy(samples_hbm, samples, sample_sem)
+    sample_load.start()
     lax.fori_loop(0, block_count, load_go, 0)
 
     barrier = pltpu.get_barrier_semaphore()
@@ -87,6 +88,7 @@
         return carry
 
     lax.fori_loop(0, block_count // 8, square_group, 0)
+    sample_load.wait()
     pl.semaphore_wait(barrier, row_count + 1)
 
     nb2 = block_count // 2
@@ -114,10 +116,10 @@
     ones = jnp.ones((sample_count, width), BF16)
 
     def slot_tile(owner, slot):
-        pair = table[(s * row_count + owner) * cap + slot]
-        active = (slot < table[count_at + s * row_count + owner]).astype(F32)
-        first = table[first_at + pair]
-        second = table[second_at + pair]
+        pair = pair_list[s, slot, owner]
+        active = (slot < pair_count[s, owner]).astype(F32)
+        first = pair_blocks[0, pair]
+        second = pair_blocks[1, pair]
         picked = samples[first].reshape(1, sample_count)
         hits = jnp.where(positions == picked, 1.0, 0.0).astype(BF16)
         multiplicity = jnp.dot(hits, ones, preferred_element_type=F32)
@@ -131,43 +133,77 @@
     def core_copy(j):
         return send(core_out.at[j], core_in.at[j], core_send.at[j], core_recv.at[j], s, partner)
 
-    def row_copy(j):
-        owner = lax.rem(s + j, row_count)
-        target = row_in.at[s, pl.ds(0, half)]
-        return send(keep.at[j], target, row_send.at[j], row_recv.at[s], owner, g)
-
-    def row_from(j):
-        source = lax.rem(s + j, row_count)
-        target = row_in.at[source, pl.ds(0, half)]
-        return send(keep.at[j], target, row_send.at[j], row_recv.at[source], source, g)
-
-    def make(j):
-        owner = lax.rem(s + j, row_count)
+    top = lax.div(s, row_half)
+
+    def far(j):
+        return (1 - top) * row_half + lax.rem(s + j, row_half)
+
+    def near(j):
+        return top * row_half + lax.rem(s + j, row_half)
+
+    mine = pl.ds(high * quota, quota)
+    theirs = pl.ds((1 - high) * quota, quota)
+
+    def high_copy(j):
+        return send(keep.at[j, theirs], high_in.at[j], high_send.at[j], high_recv.at[j], s, across)
+
+    def far_copy(j):
+        return send(keep.at[j, mine], row_in.at[s, mine], row_send.at[j], row_recv.at[s], far(j), g)
+
+    def far_from(j):
+        source = far(j)
+        return send(keep.at[j, mine], row_in.at[source, mine], row_send.at[j], row_recv.at[source], source, g)
+
+    whole = pl.ds(0, half)
+
+    def near_copy(j):
+        k = row_half + j
+        return send(keep.at[k], row_in.at[s, whole], row_send.at[k], row_recv.at[s], near(j), g)
+
+    def near_from(j):
+        k = row_half + j
+        source = near(j)
+        return send(keep.at[k], row_in.at[source, whole], row_send.at[k], row_recv.at[source], source, g)
+
+    def make(j, owner):
         for n in range(half):
             core_out[j, n] = slot_tile(owner, (1 - low) * half + n)
         core_copy(j).start()
         for n in range(half):
             keep[j, n] = slot_tile(owner, low * half + n)
 
-    def forward(j):
+    def fold(j):
         core_copy(j).wait_recv()
         keep[j] = keep[j] + core_in[j]
-        row_copy(j).start()
-
-    def step(j, carry):
-        make(j)
-        forward(j - 1)
-        return carry
-
-    cut1 = min(3, row_count)
-    cut2 = min(5, row_count)
+
+    def fold_far(j):
+        fold(j)
+        high_copy(j).start()
+
+    def cross(j):
+        high_copy(j).wait_recv()
+        keep[j, mine] = keep[j, mine] + high_in[j]
+        far_copy(j).start()
+
+    def fold_near(j):
+        fold(row_half + j)
+        near_copy(j).start()
+
     sq1.start()
-    make(1)
-    lax.fori_loop(2, cut1, step, 0)
+    make(0, far(0))
     sq1.wait()
     sq_half[...] = squares[my_half, :] + sq_in[...]
     sq2.start()
-    lax.fori_loop(cut1, cut2, step, 0)
+    make(1, far(1))
+    fold_far(0)
+
+    def far_step(j, carry):
+        make(j, far(j))
+        fold_far(j - 1)
+        cross(j - 2)
+        return carry
+
+    lax.fori_loop(2, row_half, far_step, 0)
     sq2.wait()
     sq_rows[s] = sq_half[span(high * nb4, nb4), :] + sq_in2[...]
 
@@ -176,11 +212,23 @@
         return carry
 
     lax.fori_loop(1, row_count, sq_go, 0)
-    lax.fori_loop(cut2, row_count, step, 0)
-    make(0)
-    forward(row_count - 1)
-    core_copy(0).wait_recv()
-    row_in[s, pl.ds(0, half)] = keep[0] + core_in[0]
+    fold_far(row_half - 1)
+    make(row_half + 1, near(1))
+    cross(row_half - 2)
+    make(row_half + 2, near(2))
+    fold_near(1)
+    cross(row_half - 1)
+
+    def near_step(j, carry):
+        make(row_half + j, near(j))
+        fold_near(j - 1)
+        return carry
+
+    lax.fori_loop(3, row_half, near_step, 0)
+    make(row_half, s)
+    fold_near(row_half - 1)
+    core_copy(row_half).wait_recv()
+    row_in[s, whole] = keep[row_half] + core_in[row_half]
 
     def sq_done(j, carry):
         sq_row_from(j).wait_recv()
@@ -193,21 +241,27 @@
     sq_total[quarter, :] = sq_sum
     sq4.start()
 
-    def row_done(j, carry):
-        row_from(j).wait_recv()
-        return carry
-
-    lax.fori_loop(1, row_count, row_done, 0)
+    def near_done(j, carry):
+        near_from(j).wait_recv()
+        return carry
+
+    def far_done(j, carry):
+        far_from(j).wait_recv()
+        return carry
+
+    lax.fori_loop(1, row_half, near_done, 0)
+    lax.fori_loop(0, row_half, far_done, 0)
 
     def owned(grp, n):
         pair = s * region + grp * tile_dev + n
         total = None
-        for source in range(row_count):
-            base = (source * row_count + s) * cap + low * half
+        for j in range(row_count):
+            source = far(j) if j < row_half else near(j - row_half)
             index = half
-            for m in range(half):
-                same = (table[base + m] == pair).astype(jnp.int32)
-                index = jnp.minimum(index, half - (half - m) * same)
+            for m in range(quota if j < row_half else half):
+                place = m + high * quota if j < row_half else m
+                same = (pair_list[source, low * half + place, s] == pair).astype(jnp.int32)
+                index = jnp.minimum(index, half - (half - place) * same)
             tile = row_in[source, index]
             total = tile if total is None else total + tile
         return total
@@ -227,7 +281,7 @@
         part_b[n] = part_b[n] + in_a[n]
         b_copy(n).start()
 
-    def far(n, carry):
+    def distant(n, carry):
         part_a[n] = owned(far_other, n)
         a_copy(n).start()
         part_b[n] = owned(far_low, n)
@@ -238,7 +292,7 @@
 
         return carry
 
-    lax.fori_loop(0, tile_dev, far, 0)
+    lax.fori_loop(0, tile_dev, distant, 0)
     pass_on(tile_dev - 1)
     sq4.wait()
     sq5.start()
@@ -250,11 +304,11 @@
     lax.fori_loop(0, tile_dev, near_other, 0)
     c_copy.start()
 
-    def near(n, carry):
+    def local(n, carry):
         part_d[n] = owned(g, n)
         return carry
 
-    lax.fori_loop(0, tile_dev, near, 0)
+    lax.fori_loop(0, tile_dev, local, 0)
     sq5.wait()
     c_copy.wait()
     sq_total[...] = jnp.sqrt(
@@ -263,8 +317,8 @@
 
     def finish(n, carry):
         pair = s * region + g * tile_dev + n
-        first = table[first_at + pair]
-        second = table[second_at + pair]
+        first = pair_blocks[0, pair]
+        second = pair_blocks[1, pair]
         left = jnp.broadcast_to(sq_total[first].reshape(1, width), (width, width)).T
         right = sq_total[second].reshape(1, width)
         b_copy(n).wait_recv()
@@ -283,12 +337,22 @@
 
     def drain_rows(j, carry):
         core_copy(j).wait_send()
-        row_copy(j).wait_send()
         sq_row(j).wait_send()
+        return carry
+
+    def drain_far(j, carry):
+        high_copy(j).wait_send()
+        far_copy(j).wait_send()
+        return carry
+
+    def drain_near(j, carry):
+        near_copy(j).wait_send()
         return carry
 
     lax.fori_loop(1, row_count, drain_rows, 0)
     core_copy(0).wait_send()
+    lax.fori_loop(0, row_half, drain_far, 0)
+    lax.fori_loop(1, row_half, drain_near, 0)
 
 
 def shards(matrix, sample_rows, pair_list, pair_count, pair_blocks):
@@ -301,14 +365,6 @@
     pairs = pair_blocks.shape[0]
     tile_dev = pairs // (row_count * grp_count)
     half = cap // 2
-    table = jnp.concatenate(
-        [
-            pair_list.reshape(-1),
-            pair_count.reshape(-1),
-            pair_blocks[:, 0],
-            pair_blocks[:, 1],
-        ]
-    )
     dma = pltpu.SemaphoreType.DMA
 
     def vmem(*shape):
@@ -321,12 +377,16 @@
         out_shape=jax.ShapeDtypeStruct((tile_dev, width, width), F32),
         in_specs=[
             pl.BlockSpec(memory_space=pltpu.SMEM),
-            pl.BlockSpec(memory_space=pltpu.VMEM),
+            pl.BlockSpec(memory_space=pltpu.SMEM),
+            pl.BlockSpec(memory_space=pltpu.SMEM),
+            pl.BlockSpec(memory_space=pl.ANY),
             pl.BlockSpec(memory_space=pl.ANY),
         ],
         out_specs=pl.BlockSpec(memory_space=pltpu.VMEM),
         scratch_shapes=[
             pltpu.VMEM((block_count, rows_dev, width), BF16),
+            pltpu.VMEM((block_count, sample_count), jnp.int32),
+            dma,
             vmem(block_count, width),
             vmem(nb2, width),
             vmem(nb2, width),
@@ -336,10 +396,12 @@
             vmem(row_count, half, width, width),
             vmem(row_count, half, width, width),
             vmem(row_count, half, width, width),
+            vmem(row_count // 2, half // 2, width, width),
             vmem(row_count, half + 1, width, width),
             some, some, some, some, some, some, some,
             dma((block_count,)), dma((4,)), dma((4,)), dma((row_count,)), dma((row_count,)),
-            dma((row_count,)), dma((row_count,)), dma((row_count,)), dma((row_count,)),
+            dma((row_count,)), dma((row_count,)), dma((row_count // 2,)), dma((row_count // 2,)),
+            dma((row_count,)), dma((row_count,)),
             dma((tile_dev,)), dma((tile_dev,)), dma((tile_dev,)), dma((tile_dev,)),
             dma, dma,
         ],
@@ -347,7 +409,7 @@
             collective_id=0, has_side_effects=True, vmem_limit_bytes=67043328
         ),
         name="gram_tiles",
-    )(table, sample_rows[0], matrix)
+    )(pair_list.transpose(0, 2, 1), pair_count, pair_blocks.T, sample_rows[0], matrix)
 
 
 def solution(mesh):

time: 61.2 us -> 50.3 us (0.82)
  the two profiles are of different devices: /device:TPU:11 before, /device:TPU:0 now
where the time goes in v2:
time: 50.3 us; the launch traced here: 49.4 us
  Pallas kernels  47.5 us (94%)
  local copies, waits for them, and re-layouts  1.87 us (4%)
    pallas_call x1, Pallas kernels, shards(): pl.pallas_call(functools.partial(kernel, (row_count, grp_count, cap, pair...  47.5 us
    unnamed x1, local copies, waits for them, and re-layouts  1.87 us

profile of v2, /device:TPU:0, one launch (start us, length us, event | category | flops | bytes accessed | tf_op | source)
XLA Modules:
  0.0 49.4 jit_solution(8552688678152086414)
XLA Ops:
  0.0 47.5 %gram_tiles.1 = f32[8,128,128]{2,1,0:T(8,128)} custom-call(s32[8,4,8]{2,1,0:T(4,128)} %bitcast.4, s32[8,8]{1,0:T(8,128)} %pair_count.1, s32[2,256]{1,0:T(2,128)} %bitcast.5, s32[128,256]{1,0:T(8,128)} %bitcast.3, bf16[320,16384]{1,0:T(8,128)(2,1)} %matrix.1), custom_call_target="tpu_custom_call" | custom-call | tf_op jit(solution)/shard_map/gram_tiles/pallas_call | solution.py:375
  47.5 1.9 %copy.7 = f32[8,128,128]{2,1,0:T(8,128)} copy(f32[8,128,128]{2,1,0:T(8,128)} %gram_tiles.1) | data formatting | bytes 1048576

commit v3 on v2

--- a/solution.py
+++ b/solution.py
@@ -16,7 +16,7 @@
 def kernel(
     dims, pair_list, pair_count, pair_blocks, samples_hbm, matrix, out,
     mat, samples, sample_sem, squares, sq_in, sq_half, sq_in2, sq_rows, sq_total,
-    core_out, core_in, keep, high_in, row_in, part_a, part_b, part_c, part_d, in_a, in_b, in_c,
+    core_out, core_in, keep, high_in, row_in0, row_in1, part_a, part_b, part_c, part_d, in_a, in_b, in_c,
     load_sem, sq_send, sq_recv, sq_row_send, sq_row_recv,
     core_send, core_recv, high_send, high_recv, row_send, row_recv,
     a_send, a_recv, b_send, b_recv, c_send, c_recv,
@@ -69,10 +69,14 @@
 
     lax.fori_loop(1, row_count, greet, 0)
 
-    zero_tile = jnp.zeros((width, width), F32)
+    row_in = (row_in0, row_in1)
+    tall = width // 2
+    lines_of = (pl.ds(0, tall), pl.ds(tall, tall))
+    zero_tile = jnp.zeros((tall, width), F32)
 
     def clear(j, carry):
-        row_in[j, half] = zero_tile
+        for h in range(2):
+            row_in[h][j, half] = zero_tile
         return carry
 
     lax.fori_loop(0, row_count, clear, 0)
@@ -143,92 +147,139 @@
 
     mine = pl.ds(high * quota, quota)
     theirs = pl.ds((1 - high) * quota, quota)
-
-    def high_copy(j):
-        return send(keep.at[j, theirs], high_in.at[j], high_send.at[j], high_recv.at[j], s, across)
-
-    def far_copy(j):
-        return send(keep.at[j, mine], row_in.at[s, mine], row_send.at[j], row_recv.at[s], far(j), g)
-
-    def far_from(j):
+    whole = pl.ds(0, half)
+    last = row_count - 1
+
+    def is_far(k):
+        return (k == 0) | ((lax.rem(k, 2) == 1) & (k < last))
+
+    def is_near(k):
+        return (k > 0) & (lax.rem(k, 2) == 0)
+
+    def far_at(j):
+        return jnp.maximum(2 * j - 1, 0)
+
+    def high_copy(k):
+        return send(keep.at[k, theirs], high_in.at[k], high_send.at[k], high_recv.at[k], s, across)
+
+    def far_copy(h, j):
+        k = far_at(j)
+        return send(
+            keep.at[k, mine, lines_of[h]], row_in[h].at[s, mine],
+            row_send.at[h * row_count + k], row_recv.at[h * row_count + s], far(j), g,
+        )
+
+    def far_from(h, j):
+        k = far_at(j)
         source = far(j)
-        return send(keep.at[j, mine], row_in.at[source, mine], row_send.at[j], row_recv.at[source], source, g)
-
-    whole = pl.ds(0, half)
-
-    def near_copy(j):
-        k = row_half + j
-        return send(keep.at[k], row_in.at[s, whole], row_send.at[k], row_recv.at[s], near(j), g)
-
-    def near_from(j):
-        k = row_half + j
+        return send(
+            keep.at[k, mine, lines_of[h]], row_in[h].at[source, mine],
+            row_send.at[h * row_count + k], row_recv.at[h * row_count + source], source, g,
+        )
+
+    def near_copy(h, j):
+        k = 2 * j
+        return send(
+            keep.at[k, whole, lines_of[h]], row_in[h].at[s, whole],
+            row_send.at[h * row_count + k], row_recv.at[h * row_count + s], near(j), g,
+        )
+
+    def near_from(h, j):
+        k = 2 * j
         source = near(j)
-        return send(keep.at[k], row_in.at[source, whole], row_send.at[k], row_recv.at[source], source, g)
-
-    def make(j, owner):
+        return send(
+            keep.at[k, whole, lines_of[h]], row_in[h].at[source, whole],
+            row_send.at[h * row_count + k], row_recv.at[h * row_count + source], source, g,
+        )
+
+    def owner_of(k):
+        odd = lax.rem(k, 2)
+        final = lax.div(k, last)
+        other = jnp.maximum(odd, 1 - jnp.minimum(k, 1)) * (1 - final)
+        j = lax.div(k + 1, 2) * (1 - final)
+        return (top * (1 - other) + (1 - top) * other) * row_half + lax.rem(s + j, row_half)
+
+    def make_out(k):
+        owner = owner_of(k)
         for n in range(half):
-            core_out[j, n] = slot_tile(owner, (1 - low) * half + n)
-        core_copy(j).start()
+            core_out[k, n] = slot_tile(owner, (1 - low) * half + n)
+        core_copy(k).start()
+
+    def make_keep(k):
+        owner = owner_of(k)
         for n in range(half):
-            keep[j, n] = slot_tile(owner, low * half + n)
-
-    def fold(j):
-        core_copy(j).wait_recv()
-        keep[j] = keep[j] + core_in[j]
-
-    def fold_far(j):
-        fold(j)
-        high_copy(j).start()
-
-    def cross(j):
-        high_copy(j).wait_recv()
-        keep[j, mine] = keep[j, mine] + high_in[j]
-        far_copy(j).start()
-
-    def fold_near(j):
-        fold(row_half + j)
-        near_copy(j).start()
+            keep[k, n] = slot_tile(owner, low * half + n)
+        core_copy(k).wait_recv()
+        keep[k] = keep[k] + core_in[k]
+
+    def cross(k):
+        high_copy(k).wait_recv()
+        keep[k, mine] = keep[k, mine] + high_in[k]
+        far_copy(0, lax.div(k + 1, 2)).start()
 
     sq1.start()
-    make(0, far(0))
-    sq1.wait()
-    sq_half[...] = squares[my_half, :] + sq_in[...]
-    sq2.start()
-    make(1, far(1))
-    fold_far(0)
-
-    def far_step(j, carry):
-        make(j, far(j))
-        fold_far(j - 1)
-        cross(j - 2)
-        return carry
-
-    lax.fori_loop(2, row_half, far_step, 0)
-    sq2.wait()
-    sq_rows[s] = sq_half[span(high * nb4, nb4), :] + sq_in2[...]
-
-    def sq_go(j, carry):
-        sq_row(j).start()
-        return carry
-
-    lax.fori_loop(1, row_count, sq_go, 0)
-    fold_far(row_half - 1)
-    make(row_half + 1, near(1))
-    cross(row_half - 2)
-    make(row_half + 2, near(2))
-    fold_near(1)
-    cross(row_half - 1)
-
-    def near_step(j, carry):
-        make(row_half + j, near(j))
-        fold_near(j - 1)
-        return carry
-
-    lax.fori_loop(3, row_half, near_step, 0)
-    make(row_half, s)
-    fold_near(row_half - 1)
-    core_copy(row_half).wait_recv()
-    row_in[s, whole] = keep[row_half] + core_in[row_half]
+    fold_lag, cross_lag = 2, 5
+
+    def step(i, carry):
+        @pl.when(i < row_count)
+        def _():
+            make_out(i)
+
+        @pl.when(i == 2)
+        def _():
+            sq1.wait()
+            sq_half[...] = squares[my_half, :] + sq_in[...]
+            sq2.start()
+
+        k = i - fold_lag
+
+        @pl.when((k >= 0) & (k < row_count))
+        def _():
+            make_keep(k)
+
+            @pl.when(is_far(k))
+            def _():
+                high_copy(k).start()
+
+            @pl.when(is_near(k))
+            def _():
+                near_copy(0, lax.div(k, 2)).start()
+
+        @pl.when(i == 5)
+        def _():
+            sq2.wait()
+            sq_rows[s] = sq_half[span(high * nb4, nb4), :] + sq_in2[...]
+
+            def sq_go(j, carry):
+                sq_row(j).start()
+                return carry
+
+            lax.fori_loop(1, row_count, sq_go, 0)
+
+        m = i - cross_lag
+
+        @pl.when((m >= 0) & (m < row_count))
+        def _():
+            @pl.when(is_far(m))
+            def _():
+                cross(m)
+
+        return carry
+
+    lax.fori_loop(0, row_count + cross_lag - 2, step, 0)
+
+    def second_far(j, carry):
+        far_copy(1, j).start()
+        return carry
+
+    def second_near(j, carry):
+        near_copy(1, j).start()
+        return carry
+
+    lax.fori_loop(0, row_half, second_far, 0)
+    lax.fori_loop(1, row_half, second_near, 0)
+    for h in range(2):
+        row_in[h][s, whole] = keep[last, whole, lines_of[h]]
 
     def sq_done(j, carry):
         sq_row_from(j).wait_recv()
@@ -241,18 +292,19 @@
     sq_total[quarter, :] = sq_sum
     sq4.start()
 
-    def near_done(j, carry):
-        near_from(j).wait_recv()
-        return carry
-
-    def far_done(j, carry):
-        far_from(j).wait_recv()
-        return carry
-
-    lax.fori_loop(1, row_half, near_done, 0)
-    lax.fori_loop(0, row_half, far_done, 0)
-
-    def owned(grp, n):
+    def arrive(h):
+        def near_done(j, carry):
+            near_from(h, j).wait_recv()
+            return carry
+
+        def far_done(j, carry):
+            far_from(h, j).wait_recv()
+            return carry
+
+        lax.fori_loop(1, row_half, near_done, 0)
+        lax.fori_loop(0, row_half, far_done, 0)
+
+    def owned(h, grp, n):
         pair = s * region + grp * tile_dev + n
         total = None
         for j in range(row_count):
@@ -262,78 +314,95 @@
                 place = m + high * quota if j < row_half else m
                 same = (pair_list[source, low * half + place, s] == pair).astype(jnp.int32)
                 index = jnp.minimum(index, half - (half - place) * same)
-            tile = row_in[source, index]
+            tile = row_in[h][source, index]
             total = tile if total is None else total + tile
         return total
 
-    def a_copy(n):
-        return send(part_a.at[n], in_a.at[n], a_send.at[n], a_recv.at[n], s, partner)
-
-    def b_copy(n):
-        return send(part_b.at[n], in_b.at[n], b_send.at[n], b_recv.at[n], s, across)
-
-    c_copy = send(part_c, in_c, c_send, c_recv, s, partner)
+    def a_copy(h, n):
+        k = h * tile_dev + n
+        lines = lines_of[h]
+        return send(part_a.at[n, lines], in_a.at[n, lines], a_send.at[k], a_recv.at[k], s, partner)
+
+    def b_copy(h, n):
+        k = h * tile_dev + n
+        lines = lines_of[h]
+        return send(part_b.at[n, lines], in_b.at[n, lines], b_send.at[k], b_recv.at[k], s, across)
+
+    def c_copy(h):
+        lines = lines_of[h]
+        return send(part_c.at[:, lines], in_c.at[:, lines], c_send.at[h], c_recv.at[h], s, partner)
+
     far_low = (1 - high) * 2 + low
     far_other = (1 - high) * 2 + (1 - low)
 
-    def pass_on(n):
-        a_copy(n).wait_recv()
-        part_b[n] = part_b[n] + in_a[n]
-        b_copy(n).start()
-
-    def distant(n, carry):
-        part_a[n] = owned(far_other, n)
-        a_copy(n).start()
-        part_b[n] = owned(far_low, n)
-
-        @pl.when(n > 0)
-        def _():
-            pass_on(n - 1)
-
-        return carry
-
-    lax.fori_loop(0, tile_dev, distant, 0)
-    pass_on(tile_dev - 1)
+    def combine(h):
+        lines = lines_of[h]
+
+        def pass_on(n):
+            a_copy(h, n).wait_recv()
+            part_b[n, lines] = part_b[n, lines] + in_a[n, lines]
+            b_copy(h, n).start()
+
+        def distant(n, carry):
+            @pl.when(n < tile_dev)
+            def _():
+                part_a[n, lines] = owned(h, far_other, n)
+                a_copy(h, n).start()
+                part_b[n, lines] = owned(h, far_low, n)
+
+            @pl.when(n >= 3)
+            def _():
+                pass_on(n - 3)
+
+            return carry
+
+        def near_other(n, carry):
+            part_c[n, lines] = owned(h, partner, n)
+            return carry
+
+        def local(n, carry):
+            part_d[n, lines] = owned(h, g, n)
+            return carry
+
+        lax.fori_loop(0, tile_dev + 3, distant, 0)
+        lax.fori_loop(0, tile_dev, near_other, 0)
+        c_copy(h).start()
+        lax.fori_loop(0, tile_dev, local, 0)
+
+    arrive(0)
+    combine(0)
     sq4.wait()
     sq5.start()
-
-    def near_other(n, carry):
-        part_c[n] = owned(partner, n)
-        return carry
-
-    lax.fori_loop(0, tile_dev, near_other, 0)
-    c_copy.start()
-
-    def local(n, carry):
-        part_d[n] = owned(g, n)
-        return carry
-
-    lax.fori_loop(0, tile_dev, local, 0)
+    arrive(1)
+    combine(1)
     sq5.wait()
-    c_copy.wait()
     sq_total[...] = jnp.sqrt(
         sq_total[...] / (rows_dev * row_count * grp_count) + epsilon
     )
-
-    def finish(n, carry):
-        pair = s * region + g * tile_dev + n
-        first = pair_blocks[0, pair]
-        second = pair_blocks[1, pair]
-        left = jnp.broadcast_to(sq_total[first].reshape(1, width), (width, width)).T
-        right = sq_total[second].reshape(1, width)
-        b_copy(n).wait_recv()
-        total = part_d[n] + in_c[n] + in_b[n]
-        out[n] = total / (sample_count * left * right)
-        return carry
-
-    lax.fori_loop(0, tile_dev, finish, 0)
-
-    def drain_tiles(n, carry):
-        a_copy(n).wait_send()
-        b_copy(n).wait_send()
-        return carry
-
-    lax.fori_loop(0, tile_dev, drain_tiles, 0)
+    for h in range(2):
+        lines = lines_of[h]
+        c_copy(h).wait()
+
+        def finish(n, carry):
+            pair = s * region + g * tile_dev + n
+            first = pair_blocks[0, pair]
+            second = pair_blocks[1, pair]
+            left = jnp.broadcast_to(sq_total[first].reshape(1, width), (width, width)).T
+            right = sq_total[second].reshape(1, width)
+            b_copy(h, n).wait_recv()
+            total = part_d[n, lines] + in_c[n, lines] + in_b[n, lines]
+            scale = sample_count * left[h * tall : (h + 1) * tall] * right
+            out[n, lines] = total / scale
+            return carry
+
+        lax.fori_loop(0, tile_dev, finish, 0)
+
+        def drain_tiles(n, carry):
+            a_copy(h, n).wait_send()
+            b_copy(h, n).wait_send()
+            return carry
+
+        lax.fori_loop(0, tile_dev, drain_tiles, 0)
 
     def drain_rows(j, carry):
         core_copy(j).wait_send()
@@ -341,12 +410,14 @@
         return carry
 
     def drain_far(j, carry):
-        high_copy(j).wait_send()
-        far_copy(j).wait_send()
+        high_copy(far_at(j)).wait_send()
+        for h in range(2):
+            far_copy(h, j).wait_send()
         return carry
 
     def drain_near(j, carry):
-        near_copy(j).wait_send()
+        for h in range(2):
+            near_copy(h, j).wait_send()
         return carry
 
     lax.fori_loop(1, row_count, drain_rows, 0)
@@ -396,14 +467,15 @@
             vmem(row_count, half, width, width),
             vmem(row_count, half, width, width),
             vmem(row_count, half, width, width),
-            vmem(row_count // 2, half // 2, width, width),
-            vmem(row_count, half + 1, width, width),
+            vmem(row_count, half // 2, width, width),
+            vmem(row_count, half + 1, width // 2, width),
+            vmem(row_count, half + 1, width // 2, width),
             some, some, some, some, some, some, some,
             dma((block_count,)), dma((4,)), dma((4,)), dma((row_count,)), dma((row_count,)),
-            dma((row_count,)), dma((row_count,)), dma((row_count // 2,)), dma((row_count // 2,)),
-            dma((row_count,)), dma((row_count,)),
-            dma((tile_dev,)), dma((tile_dev,)), dma((tile_dev,)), dma((tile_dev,)),
-            dma, dma,
+            dma((row_count,)), dma((row_count,)), dma((row_count,)), dma((row_count,)),
+            dma((2 * row_count,)), dma((2 * row_count,)),
+            dma((2 * tile_dev,)), dma((2 * tile_dev,)), dma((2 * tile_dev,)),
+            dma((2 * tile_dev,)), dma((2,)), dma((2,)),
         ],
         compiler_params=pltpu.CompilerParams(
             collective_id=0, has_side_effects=True, vmem_limit_bytes=67043328

time: 50.3 us -> 51.1 us (1.016); the launches traced: 49.4 us -> 50.9 us
  Pallas kernels: 47.5 us -> 49 us
    pallas_call x1, Pallas kernels: 47.5 us -> 49 us  [shards(): pl.pallas_call(functools.partial(kernel, (row_count, grp_count, cap, pair...]
where the time goes in v3:
time: 51.1 us; the launch traced here: 50.9 us
  Pallas kernels  49 us (96%)
  local copies, waits for them, and re-layouts  1.87 us (4%)
    pallas_call x1, Pallas kernels, shards(): pl.pallas_call(functools.partial(kernel, (row_count, grp_count, cap, pair...  49 us
    unnamed x1, local copies, waits for them, and re-layouts  1.87 us

profile of v3, /device:TPU:0, one launch (start us, length us, event | category | flops | bytes accessed | tf_op | source)
XLA Modules:
  0.0 50.9 jit_solution(15305392107155286003)
XLA Ops:
  0.0 49.0 %gram_tiles.1 = f32[8,128,128]{2,1,0:T(8,128)} custom-call(s32[8,4,8]{2,1,0:T(4,128)} %bitcast.4, s32[8,8]{1,0:T(8,128)} %pair_count.1, s32[2,256]{1,0:T(2,128)} %bitcast.5, s32[128,256]{1,0:T(8,128)} %bitcast.3, bf16[320,16384]{1,0:T(8,128)(2,1)} %matrix.1), custom_call_target="tpu_custom_call" | custom-call | tf_op jit(solution)/shard_map/gram_tiles/pallas_call | solution.py:446
  49.0 1.9 %copy.7 = f32[8,128,128]{2,1,0:T(8,128)} copy(f32[8,128,128]{2,1,0:T(8,128)} %gram_tiles.1) | data formatting | bytes 1048576

commit v4 on v3

--- a/solution.py
+++ b/solution.py
@@ -151,26 +151,23 @@
     last = row_count - 1
 
     def is_far(k):
-        return (k == 0) | ((lax.rem(k, 2) == 1) & (k < last))
+        return k < row_half
 
     def is_near(k):
-        return (k > 0) & (lax.rem(k, 2) == 0)
-
-    def far_at(j):
-        return jnp.maximum(2 * j - 1, 0)
+        return (k >= row_half) & (k < last)
 
     def high_copy(k):
         return send(keep.at[k, theirs], high_in.at[k], high_send.at[k], high_recv.at[k], s, across)
 
     def far_copy(h, j):
-        k = far_at(j)
+        k = j
         return send(
             keep.at[k, mine, lines_of[h]], row_in[h].at[s, mine],
             row_send.at[h * row_count + k], row_recv.at[h * row_count + s], far(j), g,
         )
 
     def far_from(h, j):
-        k = far_at(j)
+        k = j
         source = far(j)
         return send(
             keep.at[k, mine, lines_of[h]], row_in[h].at[source, mine],
@@ -178,14 +175,14 @@
         )
 
     def near_copy(h, j):
-        k = 2 * j
+        k = row_half + j - 1
         return send(
             keep.at[k, whole, lines_of[h]], row_in[h].at[s, whole],
             row_send.at[h * row_count + k], row_recv.at[h * row_count + s], near(j), g,
         )
 
     def near_from(h, j):
-        k = 2 * j
+        k = row_half + j - 1
         source = near(j)
         return send(
             keep.at[k, whole, lines_of[h]], row_in[h].at[source, whole],
@@ -193,37 +190,36 @@
         )
 
     def owner_of(k):
-        odd = lax.rem(k, 2)
-        final = lax.div(k, last)
-        other = jnp.maximum(odd, 1 - jnp.minimum(k, 1)) * (1 - final)
-        j = lax.div(k + 1, 2) * (1 - final)
+        other = 1 - lax.div(k, row_half)
+        j = k + 1 - other
         return (top * (1 - other) + (1 - top) * other) * row_half + lax.rem(s + j, row_half)
 
-    def make_out(k):
+    def make(k):
         owner = owner_of(k)
+        sent = [slot_tile(owner, (1 - low) * half + n) for n in range(half)]
+        kept = [slot_tile(owner, low * half + n) for n in range(half)]
         for n in range(half):
-            core_out[k, n] = slot_tile(owner, (1 - low) * half + n)
+            core_out[k, n] = sent[n]
         core_copy(k).start()
-
-    def make_keep(k):
-        owner = owner_of(k)
         for n in range(half):
-            keep[k, n] = slot_tile(owner, low * half + n)
+            keep[k, n] = kept[n]
+
+    def fold(k):
         core_copy(k).wait_recv()
         keep[k] = keep[k] + core_in[k]
 
     def cross(k):
         high_copy(k).wait_recv()
         keep[k, mine] = keep[k, mine] + high_in[k]
-        far_copy(0, lax.div(k + 1, 2)).start()
+        far_copy(0, k).start()
 
     sq1.start()
-    fold_lag, cross_lag = 2, 5
+    fold_lag, cross_lag = 1, 3
 
     def step(i, carry):
         @pl.when(i < row_count)
         def _():
-            make_out(i)
+            make(i)
 
         @pl.when(i == 2)
         def _():
@@ -235,7 +231,7 @@
 
         @pl.when((k >= 0) & (k < row_count))
         def _():
-            make_keep(k)
+            fold(k)
 
             @pl.when(is_far(k))
             def _():
@@ -243,7 +239,7 @@
 
             @pl.when(is_near(k))
             def _():
-                near_copy(0, lax.div(k, 2)).start()
+                near_copy(0, k - row_half + 1).start()
 
         @pl.when(i == 5)
         def _():
@@ -266,7 +262,7 @@
 
         return carry
 
-    lax.fori_loop(0, row_count + cross_lag - 2, step, 0)
+    lax.fori_loop(0, row_count + fold_lag, step, 0)
 
     def second_far(j, carry):
         far_copy(1, j).start()
@@ -410,7 +406,7 @@
         return carry
 
     def drain_far(j, carry):
-        high_copy(far_at(j)).wait_send()
+        high_copy(j).wait_send()
         for h in range(2):
             far_copy(h, j).wait_send()
         return carry

time: 51.1 us -> 46.1 us (0.902)
  Pallas kernels: 49 us -> 43.7 us
    pallas_call x1, Pallas kernels: 49 us -> 43.7 us  [shards(): pl.pallas_call(functools.partial(kernel, (row_count, grp_count, cap, pair...]
where the time goes in v4:
time: 46.1 us; the launch traced here: 45.6 us
  Pallas kernels  43.7 us (95%)
  local copies, waits for them, and re-layouts  1.87 us (4%)
    pallas_call x1, Pallas kernels, shards(): pl.pallas_call(functools.partial(kernel, (row_count, grp_count, cap, pair...  43.7 us
    unnamed x1, local copies, waits for them, and re-layouts  1.87 us

profile of v4, /device:TPU:0, one launch (start us, length us, event | category | flops | bytes accessed | tf_op | source)
XLA Modules:
  0.0 45.6 jit_solution(10447243245552844330)
XLA Ops:
  0.0 43.7 %gram_tiles.1 = f32[8,128,128]{2,1,0:T(8,128)} custom-call(s32[8,4,8]{2,1,0:T(4,128)} %bitcast.4, s32[8,8]{1,0:T(8,128)} %pair_count.1, s32[2,256]{1,0:T(2,128)} %bitcast.5, s32[128,256]{1,0:T(8,128)} %bitcast.3, bf16[320,16384]{1,0:T(8,128)(2,1)} %matrix.1), custom_call_target="tpu_custom_call" | custom-call | tf_op jit(solution)/shard_map/gram_tiles/pallas_call | solution.py:442
  43.7 1.9 %copy.7 = f32[8,128,128]{2,1,0:T(8,128)} copy(f32[8,128,128]{2,1,0:T(8,128)} %gram_tiles.1) | data formatting | bytes 1048576

commit v5 on v4

--- a/solution.py
+++ b/solution.py
@@ -221,7 +221,7 @@
         def _():
             make(i)
 
-        @pl.when(i == 2)
+        @pl.when(i == 1)
         def _():
             sq1.wait()
             sq_half[...] = squares[my_half, :] + sq_in[...]
@@ -241,7 +241,7 @@
             def _():
                 near_copy(0, k - row_half + 1).start()
 
-        @pl.when(i == 5)
+        @pl.when(i == 4)
         def _():
             sq2.wait()
             sq_rows[s] = sq_half[span(high * nb4, nb4), :] + sq_in2[...]

time: 46.1 us -> 45.6 us (0.989)
  no operation moved by 1% of the time
where the time goes in v5:
time: 45.6 us; the launch traced here: 45.2 us
  Pallas kernels  43.3 us (95%)
  local copies, waits for them, and re-layouts  1.87 us (4%)
    pallas_call x1, Pallas kernels, shards(): pl.pallas_call(functools.partial(kernel, (row_count, grp_count, cap, pair...  43.3 us
    unnamed x1, local copies, waits for them, and re-layouts  1.87 us

profile of v5, /device:TPU:0, one launch (start us, length us, event | category | flops | bytes accessed | tf_op | source)
XLA Modules:
  0.0 45.2 jit_solution(12142331262696959798)
XLA Ops:
  0.0 43.3 %gram_tiles.1 = f32[8,128,128]{2,1,0:T(8,128)} custom-call(s32[8,4,8]{2,1,0:T(4,128)} %bitcast.4, s32[8,8]{1,0:T(8,128)} %pair_count.1, s32[2,256]{1,0:T(2,128)} %bitcast.5, s32[128,256]{1,0:T(8,128)} %bitcast.3, bf16[320,16384]{1,0:T(8,128)(2,1)} %matrix.1), custom_call_target="tpu_custom_call" | custom-call | tf_op jit(solution)/shard_map/gram_tiles/pallas_call | solution.py:442
  43.3 1.9 %copy.7 = f32[8,128,128]{2,1,0:T(8,128)} copy(f32[8,128,128]{2,1,0:T(8,128)} %gram_tiles.1) | data formatting | bytes 1048576
